TPU v7x, 32 devices: a whole 2x2x4 slice. The times are simulated.
32 devices in a mesh: row: 8 (over y, x, core), col: 4 (over z).
Axes of the slice: x: 2, y: 2, z: 4, core: 2. Of those that a mesh axis runs over, the one named last changes fastest.
Arguments:
- entities: bfloat16 [2, 32768, 200], P(None, ('row', 'col')), may hold values from -2.390625 to 2.390625
- relations: bfloat16 [2, 1024, 200], replicated, may hold values from -6 to 6
- src_index: int32 [131072], P(('row', 'col')), may hold values from 0 to 4095
- dst_index: int32 [131072], P(('row', 'col')), may hold values from 0 to 8191
- rel_index: int32 [131072], P(('row', 'col')), may hold values from 0 to 1023
- neg_block: int32 [256], P(('row', 'col')), may hold values from 0 to 15
Outputs:
- edge_loss: float32 [131072], P(('row', 'col'))
- relation_grad: float32 [2, 1024, 200], P(None, ('row', 'col'))
All inputs are finite; a program needn't handle non-finite values.
Results may differ from a plain program's by a relative error of at most 0.0018.
Values may be sent and summed in bfloat16 or wider, within the bound.
A program may use at most 128 MiB of HBM per device.

v0:
```python
import jax
import jax.numpy as jnp
from jax import lax
from jax.sharding import PartitionSpec as P

NEGB = 512


def bucket_terms(picked_src, picked_dst, negatives, relations, rel_ids):
    onehot = (rel_ids[:, None] == jnp.arange(relations.shape[1], dtype=jnp.int32)[None, :]).astype(
        jnp.bfloat16
    )
    rel_re = jnp.dot(onehot, relations[0], preferred_element_type=jnp.float32)
    rel_im = jnp.dot(onehot, relations[1], preferred_element_type=jnp.float32)
    src_re = picked_src[0].astype(jnp.float32)
    src_im = picked_src[1].astype(jnp.float32)
    dst_re = picked_dst[0].astype(jnp.float32)
    dst_im = picked_dst[1].astype(jnp.float32)
    query_re = src_re * rel_re - src_im * rel_im
    query_im = src_re * rel_im + src_im * rel_re
    pos_score = jnp.sum(query_re * dst_re, 1) + jnp.sum(query_im * dst_im, 1)
    groups = negatives.shape[1]
    dim = query_re.shape[1]
    qre_b = query_re.astype(jnp.bfloat16).reshape(groups, -1, dim)
    qim_b = query_im.astype(jnp.bfloat16).reshape(groups, -1, dim)
    neg_score = jnp.einsum(
        "kcd,knd->kcn", qre_b, negatives[0], preferred_element_type=jnp.float32
    ) + jnp.einsum("kcd,knd->kcn", qim_b, negatives[1], preferred_element_type=jnp.float32)
    edge_loss = jax.nn.softplus(-pos_score) + jnp.mean(jax.nn.softplus(neg_score), -1).reshape(-1)
    weights = (jax.nn.sigmoid(neg_score) / NEGB).astype(jnp.bfloat16)
    gneg_re = jnp.einsum(
        "kcn,knd->kcd", weights, negatives[0], preferred_element_type=jnp.float32
    ).reshape(-1, dim)
    gneg_im = jnp.einsum(
        "kcn,knd->kcd", weights, negatives[1], preferred_element_type=jnp.float32
    ).reshape(-1, dim)
    pull = jax.nn.sigmoid(-pos_score)[:, None]
    grad_re = gneg_re - pull * dst_re
    grad_im = gneg_im - pull * dst_im
    term_re = (grad_re * src_re + grad_im * src_im).astype(jnp.bfloat16)
    term_im = (grad_im * src_re - grad_re * src_im).astype(jnp.bfloat16)
    dims = (((0,), (0,)), ((), ()))
    rel_grad = jnp.stack(
        [
            lax.dot_general(onehot, term_re, dims, preferred_element_type=jnp.float32),
            lax.dot_general(onehot, term_im, dims, preferred_element_type=jnp.float32),
        ],
        0,
    )
    return (edge_loss, rel_grad)


def body(entities, relations, src_index, dst_index, rel_index, neg_block):
    dim = entities.shape[2]
    source_rows = lax.all_gather(entities, "col", axis=1, tiled=True)
    picked_src = jnp.take(source_rows, src_index, axis=1)
    target_rows = lax.all_gather(entities, "row", axis=1, tiled=True)
    picked_dst = jnp.take(target_rows, dst_index, axis=1)
    negatives = jnp.take(target_rows.reshape(2, -1, NEGB, dim), neg_block, axis=1)
    edge_loss, rel_grad = bucket_terms(picked_src, picked_dst, negatives, relations, rel_index)
    row_share = lax.psum_scatter(rel_grad, "row", scatter_dimension=1, tiled=True)
    grad_share = lax.psum_scatter(row_share, "col", scatter_dimension=1, tiled=True)
    return (edge_loss, grad_share)


def solution(mesh):
    placed = (
        P(None, ("row", "col"), None),
        P(),
        P(("row", "col")),
        P(("row", "col")),
        P(("row", "col")),
        P(("row", "col")),
    )
    return jax.shard_map(
        body,
        mesh=mesh,
        in_specs=placed,
        out_specs=(P(("row", "col")), P(None, ("row", "col"), None)),
        check_vma=False,
    )
```

profile of v0, /device:TPU:0, one launch (start us, length us, event | category | flops | bytes accessed | tf_op | source)
XLA Modules:
  0.0 334.6 jit_solution(3289576555236426475)
XLA Ops:
  7.9 0.7 all-gather.5.cloned.1.call-update
  10.0 0.7 compare_and_fusion
  10.8 0.7 compare_and_fusion.1
  11.5 0.7 fusion.39
  12.2 0.7 fusion.38
  12.9 6.3 %fusion.2 = f32[4096,200]{0,1:T(8,128)} fusion(s32[4096]{0:T(1024)} %param.10, bf16[2,1024,200]{1,2,0:T(8,128)(2,1)} %param.7), kind=kOutput, calls=%fused_computation.6 | convolution fusion | flops 1681915904 | bytes 3702784 | tf_op jit(solution)/shard_map/dot_general | solution.py:14
  19.3 58.6 %all-gather.3.cloned.1.call-done = bf16[2,4096,200]{1,2,0:T(8,128)(2,1)} async-done(((bf16[2,1024,200]{1,2,0:T(8,128)(2,1)}), bf16[2,4096,200]{1,2,0:T(8,128)(2,1)}) %all-gather.3.cloned.1.call-update) | async-done | bytes 3276816 | tf_op jit(solution)/shard_map/all_gather | solution.py:55
  77.9 11.1 %copy.41 = bf16[2,4096,200]{2,0,1:T(2,128)(2,1)} copy(bf16[2,4096,200]{1,2,0:T(8,128)(2,1)} %all-gather.3.cloned.1.call-done) | data formatting | bytes 6553600 | tf_op jit(solution)/shard_map/all_gather | solution.py:55
  89.0 34.5 %gather_fusion = bf16[4096,2,200]{2,1,0:T(2,128)(2,1)} fusion(bf16[2,4096,200]{2,0,1:T(2,128)(2,1)} %copy.41, s32[4096]{0:T(1024)S(1)} %fusion.38), kind=kCustom, calls=%fused_computation | custom fusion | bytes 6569984 | tf_op jit(solution)/shard_map/jit(_take)/gather | solution.py:56
  123.5 11.1 %copy.42 = bf16[4096,2,200]{0,2,1:T(8,128)(2,1)} copy(bf16[4096,2,200]{2,1,0:T(2,128)(2,1)} %gather_fusion) | data formatting | bytes 6553600 | tf_op jit(solution)/shard_map/jit(_take)/gather | solution.py:56
  134.7 20.8 %copy.43 = bf16[2,8192,200]{2,0,1:T(2,128)(2,1)} copy(bf16[2,8192,200]{1,2,0:T(8,128)(2,1)} %all-gather.5.cloned.1.call-done) | data formatting | bytes 13107200 | tf_op jit(solution)/shard_map/all_gather | solution.py:57
  155.5 35.7 %gather_fusion.1 = bf16[4096,2,200]{2,1,0:T(2,128)(2,1)} fusion(bf16[2,8192,200]{2,0,1:T(2,128)(2,1)} %copy.43, s32[4096]{0:T(1024)S(1)} %fusion.39), kind=kCustom, calls=%fused_computation.1 | custom fusion | bytes 6569984 | tf_op jit(solution)/shard_map/jit(_take)/gather | solution.py:58
  191.2 11.0 %copy.44 = bf16[4096,2,200]{0,2,1:T(8,128)(2,1)} copy(bf16[4096,2,200]{2,1,0:T(2,128)(2,1)} %gather_fusion.1) | data formatting | bytes 6553600 | tf_op jit(solution)/shard_map/jit(_take)/gather | solution.py:58
  202.2 6.0 %copy.77 = bf16[2,25,16,8,512]{4,3,1,2,0:T(8,128)(2,1)} copy(bf16[2,25,16,8,512]{4,3,2,1,0:T(8,128)(2,1)} %bitcast.118) | data formatting | bytes 13107200 | tf_op jit(solution)/shard_map/reshape | solution.py:59
  208.2 3.6 %gather_fusion.2 = bf16[8,2,512,200]{2,3,1,0:T(8,128)(2,1)S(1)} fusion(bf16[2,16,512,200]{2,3,1,0:T(8,128)(2,1)} %bitcast.119, s32[1024]{0:T(1024)S(1)} %pad_clamp_fusion), kind=kCustom, calls=%fused_computation.2 | custom fusion | bytes 6553632 | tf_op jit(solution)/shard_map/jit(_take)/gather | solution.py:59
  212.2 1.5 copy-done
  213.7 1.0 copy-done.1
  215.9 2.2 copy-done.7
  218.1 6.6 %fusion.10 = (f32[4096]{0:T(1024)S(1)}, f32[4096]{0:T(1024)S(1)}, bf16[4096,200]{0,1:T(8,128)(2,1)}, bf16[4096,200]{0,1:T(8,128)(2,1)S(1)}) fusion(bf16[2,4096,200]{1,2,0:T(8,128)(2,1)S(1)} %get-tuple-element.20, bf16[2,4096,200]{1,2,0:T(8,128)(2,1)S(1)} %get-tuple-element.21, f32[4096,200]{0,1:T(8,128)S(1)} %copy-done.7, ...), kind=kOutput, calls=%fused_computation.31 | convolution fusion | flops 1695014912 | bytes 13565952 | tf_op jit(solution)/shard_map/dot_general | solution.py:13
  224.8 1.4 fusion.22
  226.1 3.9 %fusion.19 = (u8[512,512]{0,1:T(8,128)(4,1)S(1)}, f32[8,512,512]{1,2,0:T(8,128)S(1)}) fusion(f32[8,512,512]{1,2,0:T(8,128)S(1)} %fusion.22, bf16[2,8,512,200]{2,3,1,0:T(8,128)(2,1)S(1)} %fusion.18, bf16[25,8,8,512]{3,2,1,0:T(8,128)(2,1)} %bitcast.124), kind=kOutput, calls=%fused_computation.44 | convolution fusion | flops 851181568 | bytes 20316160 | tf_op jit(solution)/shard_map/kcd,knd->kcn/dot_general | solution.py:28
  230.0 7.1 %multiply_convert_fusion = (bf16[8,512,512]{1,2,0:T(8,128)(2,1)S(1)}, f32[8,512]{1,0:T(8,128)S(1)}) fusion(f32[8,512,512]{1,2,0:T(8,128)S(1)} %get-tuple-element.19, u8[512,512]{0,1:T(8,128)(4,1)S(1)} %get-tuple-element.18), kind=kLoop, calls=%fused_computation.10 | loop fusion | flops 31453184 | bytes 12861440 | tf_op jit(solution)/shard_map/convert_element_type | solution.py:30
  237.1 1.0 convolution_bitcast_fusion.1
  238.2 1.0 convolution_bitcast_fusion
  240.7 0.9 copy-done.3
  241.6 4.4 %fusion.27 = f32[1,1024,200]{1,2,0:T(8,128)S(1)} fusion(f32[4096,200]{0,1:T(8,128)S(1)} %bitcast.122, f32[4096,200]{0,1:T(8,128)S(1)} %bitcast.120, f32[4096]{0:T(1024)S(1)} %get-tuple-element.16, s32[4096]{0:T(1024)S(1)} %copy-done.5, bf16[2,4096,200]{1,2,0:T(8,128)(2,1)S(1)} %get-tuple-element.20, bf16[2,4096,200]{1,2,0:T(8,128)(2,1)S(1)} %copy-done.3), kind=kOutput, calls=%fused_computation.59 | convolution fusion | flops 1691746304 | bytes 13959168 | tf_op jit(solution)/shard_map/dot_general | solution.py:45
  246.0 4.4 %fusion.30 = f32[1,1024,200]{1,2,0:T(8,128)S(1)} fusion(f32[4096,200]{0,1:T(8,128)S(1)} %bitcast.123, f32[4096,200]{0,1:T(8,128)S(1)} %bitcast.121, f32[4096]{0:T(1024)S(1)} %get-tuple-element.16, s32[4096]{0:T(1024)S(1)} %copy-done.5, bf16[2,4096,200]{1,2,0:T(8,128)(2,1)S(1)} %get-tuple-element.20, bf16[2,4096,200]{1,2,0:T(8,128)(2,1)S(1)} %copy-done.3), kind=kOutput, calls=%fused_computation.60 | convolution fusion | flops 1691746304 | bytes 13959168 | tf_op jit(solution)/shard_map/dot_general | solution.py:46
  250.4 1.3 pad_maximum_fusion
  251.8 36.9 %reduce-scatter.2.cloned.1.call-done = f32[2,128,200]{1,2,0:T(8,128)} async-done(((f32[2,1024,200]{1,2,0:T(8,128)}), f32[2,128,200]{1,2,0:T(8,128)}) %reduce-scatter.2.cloned.1.call-update) | async-done | bytes 204816 | tf_op jit(solution)/shard_map/reduce_scatter | solution.py:61
  288.7 1.8 copy.53
  291.8 34.8 %all-reduce.3.cloned.1.call-done = f32[2,128,200]{2,0,1:T(2,128)} async-done(((f32[2,128,200]{2,0,1:T(2,128)}), f32[2,128,200]{2,0,1:T(2,128)}) %all-reduce.3.cloned.1.call-update) | async-done | bytes 204816
  326.6 0.8 constant_dynamic-slice_fusion
  (32 shorter events, 6.3 us)
Async XLA Ops:
  7.2 70.7 %all-gather.3.cloned.1.call-start = ((), (), s32[]{:S(2)}) async-start(), calls=%async_computation.1 | async-start | bytes 4096000 | tf_op jit(solution)/shard_map/all_gather | solution.py:55
  7.9 126.8 %all-gather.5.cloned.1.call-start = ((), (), s32[]{:S(2)}) async-start(), calls=%async_computation.2 | async-start | bytes 7372800 | tf_op jit(solution)/shard_map/all_gather | solution.py:57
  8.6 280.1 %reduce-scatter.2.cloned.1.call-start = ((), (), s32[]{:S(2)}) async-start(), calls=%async_computation.3 | async-start | bytes 1843200 | tf_op jit(solution)/shard_map/reduce_scatter | solution.py:61
  211.8 1.9 copy-start
  211.8 2.9 copy-start.1
  214.7 1.1 copy-start.4
  214.7 1.1 copy-start.5
  214.7 3.4 %copy-start.7 = (f32[4096,200]{0,1:T(8,128)S(1)}, f32[4096,200]{0,1:T(8,128)}, u32[]{:S(2)}) copy-start(f32[4096,200]{0,1:T(8,128)} %fusion.2) | copy-start | bytes 9830404
  215.4 9.4 %copy-start.2 = (bf16[2,4096,200]{1,2,0:T(8,128)(2,1)}, bf16[2,4096,200]{1,2,0:T(8,128)(2,1)S(1)}, u32[]{:S(2)}) copy-start(bf16[2,4096,200]{1,2,0:T(8,128)(2,1)S(1)} %get-tuple-element.21) | copy-start | bytes 9830404
  239.6 1.9 copy-start.3
  250.4 40.1 %copy-start.6 = (u32[32]{0:T(128)S(1)}, u32[32]{0:T(128)}, u32[]{:S(2)}) copy-start(u32[32]{0:T(128)} %constant.61) | copy-start | bytes 388
  251.7 74.8 %all-reduce.3.cloned.1.call-start = ((), (), s32[]{:S(2)}) async-start(), calls=%async_computation.4 | async-start | bytes 524288
Sparse Core Ops, SparseCore 0:
  9.5 68.3 all-gather.2
  79.8 45.1 all-gather.4
  251.8 36.8 reduce-scatter.1
  290.9 35.6 all-reduce.2
where the time goes:
time: 337 us; the launch traced here: 335 us
  local copies, waits for them, and re-layouts  145 us (43%)
  waiting for transfers between devices  132 us (39%)
  matrix products  29.1 us (9%)
  between operations  14.6 us (4%)
  other arithmetic  14.3 us (4%)
    all_gather x1, waiting for transfers between devices, body(): source_rows = lax.all_gather(entities, 'col', axis=1, tiled=True)  58.6 us
    gather x2, local copies, waits for them, and re-layouts, body(): picked_dst = jnp.take(target_rows, dst_index, axis=1)  46.7 us
    gather x2, local copies, waits for them, and re-layouts, body(): picked_src = jnp.take(source_rows, src_index, axis=1)  45.7 us
    reduce_scatter x1, waiting for transfers between devices, body(): lax.psum_scatter(rel_grad, 'row', scatter_dimension=1, tiled=True)  36.9 us
    unnamed x5, waiting for transfers between devices  36.2 us
    all_gather x1, local copies, waits for them, and re-layouts, body(): target_rows = lax.all_gather(entities, 'row', axis=1, tiled=True)  20.8 us
    all_gather x1, local copies, waits for them, and re-layouts, body(): source_rows = lax.all_gather(entities, 'col', axis=1, tiled=True)  11.1 us
    unnamed x20, local copies, waits for them, and re-layouts  8.24 us
  transfers between devices with their start and end apart: 4, of which 3 were waited for; matrix products, arithmetic and copies ran while one was open for 20% of the time, Pallas kernels for 0%

commit v1 on v0

--- a/solution.py
+++ b/solution.py
@@ -1,9 +1,374 @@
+import functools
+
 import jax
 import jax.numpy as jnp
 from jax import lax
+from jax.experimental import pallas as pl
+from jax.experimental.pallas import tpu as pltpu
 from jax.sharding import PartitionSpec as P
 
 NEGB = 512
+LANE = 128
+WIDE = 256
+VMEM_CAP = 67_043_328
+MESH = pl.DeviceIdType.MESH
+F32 = jnp.float32
+BF16 = jnp.bfloat16
+
+
+def spread_kernel(n_row, n_col, ent, src_out, dst_out, loc_sem, col_s, col_r, row_s, row_r, pair_s, pair_r):
+    r, c = lax.axis_index("row"), lax.axis_index("col")
+    chips = n_row // 2
+    chip, core = r // 2, r % 2
+    mate = chip * 2 + (1 - core)
+
+    barrier = pltpu.get_barrier_semaphore()
+    peers = [(r, (c + k) % n_col) for k in range(1, n_col)]
+    peers += [(((chip + k) % chips) * 2 + core, c) for k in range(1, chips)]
+    peers += [(mate, c)]
+    for peer in peers:
+        pl.semaphore_signal(barrier, inc=1, device_id=peer, device_id_type=MESH)
+    pl.semaphore_wait(barrier, len(peers))
+
+    sends = []
+    for k in range(1, max(n_col, chips)):
+        if k < n_col:
+            sends.append(
+                pltpu.make_async_remote_copy(
+                    src_ref=ent, dst_ref=src_out.at[c], send_sem=col_s.at[k], recv_sem=col_r.at[k],
+                    device_id=(r, (c + k) % n_col), device_id_type=MESH,
+                )
+            )
+        if k < chips:
+            sends.append(
+                pltpu.make_async_remote_copy(
+                    src_ref=ent, dst_ref=dst_out.at[r], send_sem=row_s.at[k], recv_sem=row_r.at[k],
+                    device_id=(((chip + k) % chips) * 2 + core, c), device_id_type=MESH,
+                )
+            )
+    sends.append(
+        pltpu.make_async_remote_copy(
+            src_ref=ent, dst_ref=dst_out.at[r], send_sem=pair_s.at[0], recv_sem=pair_r.at[0],
+            device_id=(mate, c), device_id_type=MESH,
+        )
+    )
+    for send in sends:
+        send.start()
+    local = [
+        pltpu.make_async_copy(ent, src_out.at[c], loc_sem.at[0]),
+        pltpu.make_async_copy(ent, dst_out.at[r], loc_sem.at[1]),
+    ]
+    for copy in local:
+        copy.start()
+    relays = []
+    for k in range(1, chips):
+        origin = ((chip + chips - k) % chips) * 2 + core
+        pltpu.make_async_remote_copy(
+            src_ref=ent, dst_ref=dst_out.at[origin], send_sem=row_s.at[k], recv_sem=row_r.at[k],
+            device_id=(mate, c), device_id_type=MESH,
+        ).wait_recv()
+        relay = pltpu.make_async_remote_copy(
+            src_ref=dst_out.at[origin], dst_ref=dst_out.at[origin], send_sem=pair_s.at[k], recv_sem=pair_r.at[k],
+            device_id=(mate, c), device_id_type=MESH,
+        )
+        relay.start()
+        relays.append(relay)
+    for k in range(1, n_col):
+        pltpu.make_async_remote_copy(
+            src_ref=ent, dst_ref=src_out.at[(c + n_col - k) % n_col], send_sem=col_s.at[k], recv_sem=col_r.at[k],
+            device_id=(mate, c), device_id_type=MESH,
+        ).wait_recv()
+    for send in sends:
+        send.wait_send()
+    sends[-1].wait_recv()
+    for relay in relays:
+        relay.wait()
+    for copy in local:
+        copy.wait()
+
+
+def spread(n_row, n_col, ent):
+    chips = n_row // 2
+    dma = pltpu.SemaphoreType.DMA
+    return pl.pallas_call(
+        functools.partial(spread_kernel, n_row, n_col),
+        name="spread",
+        out_shape=(
+            jax.ShapeDtypeStruct((n_col,) + ent.shape, ent.dtype),
+            jax.ShapeDtypeStruct((n_row,) + ent.shape, ent.dtype),
+        ),
+        in_specs=[pl.BlockSpec(memory_space=pltpu.VMEM)],
+        out_specs=(pl.BlockSpec(memory_space=pltpu.HBM), pl.BlockSpec(memory_space=pltpu.HBM)),
+        scratch_shapes=[
+            dma((2,)), dma((n_col,)), dma((n_col,)), dma((chips,)), dma((chips,)), dma((chips,)), dma((chips,)),
+        ],
+        compiler_params=pltpu.CompilerParams(collective_id=0, has_side_effects=True),
+    )(ent)
+
+
+def gather_sum_kernel(n_row, n_col, acc, out, pair_buf, sums, got, pair_s, pair_r, far_s, far_r):
+    r, c = lax.axis_index("row"), lax.axis_index("col")
+    chips = n_row // 2
+    chip, core = r // 2, r % 2
+    mate = chip * 2 + (1 - core)
+    steps = [(a, b) for a in range(chips) for b in range(n_col) if a or b]
+    goal = lambda a, b: (((chip + a) % chips) * 2 + core, (c + b) % n_col)
+
+    barrier = pltpu.get_barrier_semaphore()
+    for a, b in steps:
+        pl.semaphore_signal(barrier, inc=1, device_id=goal(a, b), device_id_type=MESH)
+    pl.semaphore_signal(barrier, inc=1, device_id=(mate, c), device_id_type=MESH)
+    pl.semaphore_wait(barrier, len(steps) + 1)
+
+    pairs = []
+    for j in range(chips):
+        copy = pltpu.make_async_remote_copy(
+            src_ref=acc.at[j, 1 - core], dst_ref=pair_buf.at[j], send_sem=pair_s.at[j], recv_sem=pair_r.at[j],
+            device_id=(mate, c), device_id_type=MESH,
+        )
+        copy.start()
+        pairs.append(copy)
+    for j in range(chips):
+        pairs[j].wait_recv()
+        sums[j] = acc[j, core] + pair_buf[j]
+    sends = []
+    for a, b in steps:
+        send = pltpu.make_async_remote_copy(
+            src_ref=sums.at[(chip + a) % chips, (c + b) % n_col], dst_ref=got.at[a, b],
+            send_sem=far_s.at[a, b], recv_sem=far_r.at[a, b],
+            device_id=goal(a, b), device_id_type=MESH,
+        )
+        send.start()
+        sends.append(send)
+    total = sums[chip, c]
+    for send, (a, b) in zip(sends, steps):
+        send.wait_recv()
+        total = total + got[a, b]
+    width = out.shape[2]
+    out[0] = total[:, :width]
+    out[1] = total[:, WIDE : WIDE + width]
+    for send in sends:
+        send.wait_send()
+    for copy in pairs:
+        copy.wait_send()
+
+
+def gather_sum(n_row, n_col, acc, dim):
+    chips = n_row // 2
+    rows = acc.shape[0] // (n_row * n_col)
+    wide = acc.shape[1]
+    dma = pltpu.SemaphoreType.DMA
+    return pl.pallas_call(
+        functools.partial(gather_sum_kernel, n_row, n_col),
+        name="gather_sum",
+        out_shape=jax.ShapeDtypeStruct((2, rows, dim), F32),
+        in_specs=[pl.BlockSpec(memory_space=pltpu.VMEM)],
+        out_specs=pl.BlockSpec(memory_space=pltpu.VMEM),
+        scratch_shapes=[
+            pltpu.VMEM((chips, n_col, rows, wide), F32),
+            pltpu.VMEM((chips, n_col, rows, wide), F32),
+            pltpu.VMEM((chips, n_col, rows, wide), F32),
+            dma((chips,)), dma((chips,)), dma((chips, n_col)), dma((chips, n_col)),
+        ],
+        compiler_params=pltpu.CompilerParams(collective_id=1, has_side_effects=True),
+    )(acc.reshape(chips, 2, n_col, rows, wide))
+
+
+def edge_kernel(
+    group, src_i, dst_i, rel_i, neg_i, rel_row, rel_tab, src_all, dst_all,
+    loss, acc, stage, s_tab, o_tab, w_tab, gs, go, gw, neg, qb, pos, term, stage_sem, neg_sem,
+):
+    n_src, n_dst = src_all.shape[0], dst_all.shape[0]
+    ent = src_all.shape[2]
+    n_rel = rel_tab.shape[1]
+    groups = neg_i.shape[0]
+    per = ent // NEGB
+    sub = 128
+
+    def neg_copy(g):
+        b = neg_i[g]
+        return pltpu.make_async_copy(
+            dst_all.at[b // per, :, pl.ds(pl.multiple_of((b % per) * NEGB, NEGB), NEGB), :],
+            neg.at[g % 2], neg_sem.at[g % 2],
+        )
+
+    def fill(table, base, read, rows):
+        def step(i, carry):
+            row = pl.multiple_of(i * sub, sub)
+            for part in range(2):
+                for half in range(2):
+                    piece = read(part, row, half).astype(F32)
+                    table[pl.ds(base + row * 4 + part * 2 + half, sub, stride=4), :] = piece
+            return carry
+
+        lax.fori_loop(0, rows // sub, step, 0)
+
+    def load(all_ref, table, count):
+        def copy(i):
+            return pltpu.make_async_copy(all_ref.at[i], stage.at[i % 2], stage_sem.at[i % 2])
+
+        copy(0).start()
+
+        def step(i, carry):
+            @pl.when(i + 1 < count)
+            def _():
+                copy(i + 1).start()
+
+            copy(i).wait()
+            slot = i % 2
+            fill(
+                table, i * (ent * 4),
+                lambda part, row, half: stage[slot, part, pl.ds(row, sub), half * LANE : (half + 1) * LANE], ent,
+            )
+            return carry
+
+        lax.fori_loop(0, count, step, 0)
+
+    neg_copy(0).start()
+    fill(w_tab, 0, lambda part, row, half: rel_tab[part, pl.ds(row, sub), half * LANE : (half + 1) * LANE], n_rel)
+    load(src_all, s_tab, n_src)
+    load(dst_all, o_tab, n_dst)
+
+    eye = lax.broadcasted_iota(jnp.int32, (sub, LANE), 0) == lax.broadcasted_iota(jnp.int32, (sub, LANE), 1)
+    nt = (((1,), (1,)), ((), ()))
+
+    def one_group(g, carry):
+        @pl.when(g + 1 < groups)
+        def _():
+            neg_copy(g + 1).start()
+
+        def pick(i, inner):
+            got = []
+            for u in range(8):
+                e = i * 8 + u
+                a = pl.multiple_of(src_i[g * group + e] * 4, 4)
+                b = pl.multiple_of(dst_i[g * group + e] * 4, 4)
+                k = pl.multiple_of(rel_i[g * group + e] * 4, 4)
+                got.append((s_tab[pl.ds(a, 4), :], o_tab[pl.ds(b, 4), :], w_tab[pl.ds(k, 4), :]))
+            for u in range(8):
+                at = pl.ds(pl.multiple_of((i * 8 + u) * 4, 4), 4)
+                gs[at, :], go[at, :], gw[at, :] = got[u]
+            return inner
+
+        lax.fori_loop(0, group // 8, pick, 0)
+
+        qrows = 32
+
+        def query(i, inner):
+            row = pl.multiple_of(i * qrows, qrows)
+            score = None
+            for half in range(2):
+                part = lambda ref, p: ref[pl.ds(row * 4 + p * 2 + half, qrows, stride=4), :]
+                sr, si, wr, wi = part(gs, 0), part(gs, 1), part(gw, 0), part(gw, 1)
+                qr = sr * wr - si * wi
+                qi = sr * wi + si * wr
+                add = qr * part(go, 0) + qi * part(go, 1)
+                score = add if score is None else score + add
+                qb[pl.ds(row, qrows), half * LANE : (half + 1) * LANE] = qr.astype(BF16)
+                qb[pl.ds(row, qrows), WIDE + half * LANE : WIDE + (half + 1) * LANE] = qi.astype(BF16)
+            pos[pl.ds(row, qrows), :] = jnp.sum(score, 1, keepdims=True)
+            return inner
+
+        lax.fori_loop(0, group // qrows, query, 0)
+        neg_copy(g).wait()
+        slot = g % 2
+
+        def block(i, inner):
+            row = pl.multiple_of(i * sub, sub)
+            rows = pl.ds(row, sub)
+            n_re, n_im = neg[slot, 0], neg[slot, 1]
+            score = lax.dot_general(qb[rows, :WIDE], n_re, nt, preferred_element_type=F32)
+            score = score + lax.dot_general(qb[rows, WIDE:], n_im, nt, preferred_element_type=F32)
+            small = jnp.exp(-jnp.abs(score))
+            soft = jnp.maximum(score, 0.0) + jnp.log1p(small)
+            weight = (jnp.where(score >= 0.0, 1.0, small) / (1.0 + small) * (1.0 / NEGB)).astype(BF16)
+            p = pos[rows, :]
+            p_small = jnp.exp(-jnp.abs(p))
+            value = jnp.maximum(-p, 0.0) + jnp.log1p(p_small) + jnp.sum(soft, 1, keepdims=True) * (1.0 / NEGB)
+            pull = jnp.where(p >= 0.0, p_small, 1.0) / (1.0 + p_small)
+            loss[pl.ds(g * (group // sub) + i, 1), :] = jnp.sum(jnp.where(eye, value, 0.0), 0, keepdims=True)
+            g_re = jnp.dot(weight, n_re, preferred_element_type=F32)
+            g_im = jnp.dot(weight, n_im, preferred_element_type=F32)
+            for half in range(2):
+                part = lambda ref, q: ref[pl.ds(row * 4 + q * 2 + half, sub, stride=4), :]
+                cols = slice(half * LANE, (half + 1) * LANE)
+                d_re = g_re[:, cols] - pull * part(go, 0)
+                d_im = g_im[:, cols] - pull * part(go, 1)
+                s_re, s_im = part(gs, 0), part(gs, 1)
+                at = pl.ds(pl.multiple_of(g * group + row, sub), sub)
+                term[at, half * LANE : (half + 1) * LANE] = (d_re * s_re + d_im * s_im).astype(BF16)
+                term[at, WIDE + half * LANE : WIDE + (half + 1) * LANE] = (d_im * s_re - d_re * s_im).astype(BF16)
+            return inner
+
+        lax.fori_loop(0, group // sub, block, 0)
+        return carry
+
+    lax.fori_loop(0, groups, one_group, 0)
+
+    tile = 256
+    edges = term.shape[0]
+
+    def reduce(i, carry):
+        row = pl.multiple_of(i * tile, tile)
+        ids = lax.broadcasted_iota(jnp.int32, (tile, edges), 0) + row
+        hot = jnp.where(ids == rel_row[...], 1.0, 0.0).astype(BF16)
+        acc[pl.ds(row, tile), :] = jnp.dot(hot, term[...], preferred_element_type=F32)
+        return carry
+
+    lax.fori_loop(0, n_rel // tile, reduce, 0)
+
+
+def edge_terms(src_all, dst_all, relations, src_index, dst_index, rel_index, neg_block):
+    edges, groups = src_index.shape[0], neg_block.shape[0]
+    group = edges // groups
+    n_rel = relations.shape[1]
+    ent = src_all.shape[2]
+    smem = pl.BlockSpec(memory_space=pltpu.SMEM)
+    vmem = pl.BlockSpec(memory_space=pltpu.VMEM)
+    hbm = pl.BlockSpec(memory_space=pltpu.HBM)
+    quad = 4
+    return pl.pallas_call(
+        functools.partial(edge_kernel, group),
+        name="edge_terms",
+        out_shape=(
+            jax.ShapeDtypeStruct((edges // LANE, LANE), F32),
+            jax.ShapeDtypeStruct((n_rel, 2 * WIDE), F32),
+        ),
+        in_specs=[smem, smem, smem, smem, vmem, vmem, hbm, hbm],
+        out_specs=(vmem, vmem),
+        scratch_shapes=[
+            pltpu.VMEM((2, 2, ent, WIDE), BF16),
+            pltpu.VMEM((src_all.shape[0] * ent * quad, LANE), F32),
+            pltpu.VMEM((dst_all.shape[0] * ent * quad, LANE), F32),
+            pltpu.VMEM((n_rel * quad, LANE), F32),
+            pltpu.VMEM((group * quad, LANE), F32),
+            pltpu.VMEM((group * quad, LANE), F32),
+            pltpu.VMEM((group * quad, LANE), F32),
+            pltpu.VMEM((2, 2, NEGB, WIDE), BF16),
+            pltpu.VMEM((group, 2 * WIDE), BF16),
+            pltpu.VMEM((group, 1), F32),
+            pltpu.VMEM((edges, 2 * WIDE), BF16),
+            pltpu.SemaphoreType.DMA((2,)),
+            pltpu.SemaphoreType.DMA((2,)),
+        ],
+        compiler_params=pltpu.CompilerParams(vmem_limit_bytes=62 * 2**20),
+    )(
+        src_index, dst_index, rel_index, neg_block, rel_index.reshape(1, edges), relations, src_all, dst_all,
+    )
+
+
+def body(n_row, n_col, entities, relations, src_index, dst_index, rel_index, neg_block):
+    dim = entities.shape[2]
+    ent = entities.shape[1]
+    pad = ((0, 0), (0, 0), (0, WIDE - dim))
+    if (n_row + n_col) * ent * 4 * LANE * 4 > 36 * 2**20:
+        return wide_body(entities, relations, src_index, dst_index, rel_index, neg_block)
+    src_all, dst_all = spread(n_row, n_col, jnp.pad(entities, pad))
+    edge_loss, acc = edge_terms(
+        src_all, dst_all, jnp.pad(relations, pad), src_index, dst_index, rel_index, neg_block
+    )
+    grad = gather_sum(n_row, n_col, acc, dim)
+    return edge_loss.reshape(-1), grad
 
 
 def bucket_terms(picked_src, picked_dst, negatives, relations, rel_ids):
@@ -50,7 +415,7 @@
     return (edge_loss, rel_grad)
 
 
-def body(entities, relations, src_index, dst_index, rel_index, neg_block):
+def wide_body(entities, relations, src_index, dst_index, rel_index, neg_block):
     dim = entities.shape[2]
     source_rows = lax.all_gather(entities, "col", axis=1, tiled=True)
     picked_src = jnp.take(source_rows, src_index, axis=1)
@@ -73,7 +438,7 @@
         P(("row", "col")),
     )
     return jax.shard_map(
-        body,
+        functools.partial(body, mesh.shape["row"], mesh.shape["col"]),
         mesh=mesh,
         in_specs=placed,
         out_specs=(P(("row", "col")), P(None, ("row", "col"), None)),

time: 337 us -> 201 us (0.60)
  Pallas kernels: 0 us -> 194 us
  local copies, waits for them, and re-layouts: 145 us -> 5.89 us
  waiting for transfers between devices: 132 us -> 0 us
  matrix products: 29.1 us -> 0 us
  other arithmetic: 14.3 us -> 0 us
  between operations: 14.6 us -> 0.68 us
    pallas_call x0 -> x3, Pallas kernels: none -> 194 us  [the longest x1 77 us: spread(): pl.pallas_call(functools.partial(spread_kernel, n_row, n_col), name='spre...]
    gather x5 -> x0, local copies, waits for them, and re-layouts: 96 us -> none  [the longest x2 46.7 us: body(): picked_dst = jnp.take(target_rows, dst_index, axis=1)]
    all_gather x2 -> x0, waiting for transfers between devices: 58.6 us -> none  [the longest x1 58.6 us: body(): source_rows = lax.all_gather(entities, 'col', axis=1, tiled=True)]
    reduce_scatter x1 -> x0, waiting for transfers between devices: 36.9 us -> none  [body(): lax.psum_scatter(rel_grad, 'row', scatter_dimension=1, tiled=True)]
    unnamed x5 -> x0, waiting for transfers between devices: 36.2 us -> none
    all_gather x2 -> x0, local copies, waits for them, and re-layouts: 31.9 us -> none  [the longest x1 20.8 us: body(): target_rows = lax.all_gather(entities, 'row', axis=1, tiled=True)]
    dot_general x8 -> x0, matrix products: 29.1 us -> none  [the longest x1 6.65 us: bucket_terms(): rel_re = jnp.dot(onehot, relations[0], preferred_element_type=jnp.float32)]
    convert_element_type x1 -> x0, other arithmetic: 7.14 us -> none  [bucket_terms(): weights = (jax.nn.sigmoid(neg_score) / NEGB).astype(jnp.bfloat16)]
  transfers between devices with their start and end apart: 4 -> 0, of which waited for: 3 -> 0; matrix products, arithmetic and copies ran while one was open for 20% -> 0% of each run, Pallas kernels for 0% -> 0%
where the time goes in v1:
time: 201 us; the launch traced here: 200 us
  Pallas kernels  194 us (97%)
  local copies, waits for them, and re-layouts  5.89 us (3%)
    pallas_call x1, Pallas kernels, spread(): pl.pallas_call(functools.partial(spread_kernel, n_row, n_col), name='spre...  77 us
    pallas_call x1, Pallas kernels, edge_terms(): pl.pallas_call(functools.partial(edge_kernel, group), name='edge_terms',...  65.9 us
    pallas_call x1, Pallas kernels, gather_sum(): pl.pallas_call(functools.partial(gather_sum_kernel, n_row, n_col), name='...  50.6 us

profile of v1, /device:TPU:0, one launch (start us, length us, event | category | flops | bytes accessed | tf_op | source)
XLA Modules:
  0.0 200.1 jit_solution(13060349689212988968)
XLA Ops:
  0.6 0.0 copy-start
  0.6 1.5 copy.9
  2.2 1.2 pad.8.ent
  3.4 0.0 copy-done
  3.4 0.5 copy.8
  3.9 1.2 pad.7.rel_tab
  5.1 77.0 %spread.1 = (bf16[4,2,1024,256]{3,2,1,0:T(8,128)(2,1)}, bf16[8,2,1024,256]{3,2,1,0:T(8,128)(2,1)}) custom-call(bf16[2,1024,256]{2,1,0:T(8,128)(2,1)} %pad.8.ent), custom_call_target="tpu_custom_call" | custom-call | tf_op jit(solution)/shard_map/spread/pallas_call | solution.py:93
  82.1 65.9 %edge_terms.1 = (f32[32,128]{1,0:T(8,128)}, f32[1024,512]{1,0:T(8,128)}) custom-call(s32[4096]{0:T(1024)} %src_i.1, s32[4096]{0:T(1024)} %dst_i.1, s32[4096]{0:T(1024)} %rel_i.1, s32[8]{0:T(128)} %neg_i.1, s32[1,4096]{1,0:T(1,128)} %bitcast.4, bf16[2,1024,256]{2,1,0:T(8,128)(2,1)} %pad.7.rel_tab, bf16[4,2,1024,256]{3,2,1,0:T(8,128)(2,1)} %get-tuple-element.6.src_all, ...), custom_call_target="tpu_custom_call" | custom-call | tf_op jit(solution)/shard_map/edge_terms/pallas_call | solution.py:330
  148.0 50.6 %gather_sum.1 = f32[2,32,200]{2,1,0:T(8,128)} custom-call(f32[4,2,4,32,512]{4,3,2,1,0:T(8,128)} %bitcast.3), custom_call_target="tpu_custom_call" | custom-call | tf_op jit(solution)/shard_map/gather_sum/pallas_call | solution.py:161
  198.6 1.5 copy.11
Async XLA Ops:
  0.6 2.7 %copy-start = (bf16[2,1024,200]{1,2,0:T(8,128)(2,1)S(1)}, bf16[2,1024,200]{1,2,0:T(8,128)(2,1)}, u32[]{:S(2)}) copy-start(bf16[2,1024,200]{1,2,0:T(8,128)(2,1)} %param.7) | copy-start | bytes 2457604

commit v2 on v1

--- a/solution.py
+++ b/solution.py
@@ -10,88 +10,104 @@
 NEGB = 512
 LANE = 128
 WIDE = 256
-VMEM_CAP = 67_043_328
 MESH = pl.DeviceIdType.MESH
 F32 = jnp.float32
 BF16 = jnp.bfloat16
 
 
-def spread_kernel(n_row, n_col, ent, src_out, dst_out, loc_sem, col_s, col_r, row_s, row_r, pair_s, pair_r):
+def spread_kernel(n_col, ent, src_out, dst_out, loc_sem, send_sem, recv_sem):
     r, c = lax.axis_index("row"), lax.axis_index("col")
-    chips = n_row // 2
     chip, core = r // 2, r % 2
-    mate = chip * 2 + (1 - core)
+    y, x = chip // 2, chip % 2
+    row_of = lambda yy, xx: (yy * 2 + xx) * 2 + core
+    xr, yr, dr = row_of(y, 1 - x), row_of(1 - y, x), row_of(1 - y, 1 - x)
+    up, down, across = (c + 1) % n_col, (c + n_col - 1) % n_col, (c + 2) % n_col
+    mate = (chip * 2 + (1 - core), c)
+    above, below, xp, yp = (r, up), (r, down), (xr, c), (yr, c)
 
     barrier = pltpu.get_barrier_semaphore()
-    peers = [(r, (c + k) % n_col) for k in range(1, n_col)]
-    peers += [(((chip + k) % chips) * 2 + core, c) for k in range(1, chips)]
-    peers += [(mate, c)]
+    peers = [mate, above, below, xp, yp]
     for peer in peers:
         pl.semaphore_signal(barrier, inc=1, device_id=peer, device_id_type=MESH)
     pl.semaphore_wait(barrier, len(peers))
 
-    sends = []
-    for k in range(1, max(n_col, chips)):
-        if k < n_col:
-            sends.append(
-                pltpu.make_async_remote_copy(
-                    src_ref=ent, dst_ref=src_out.at[c], send_sem=col_s.at[k], recv_sem=col_r.at[k],
-                    device_id=(r, (c + k) % n_col), device_id_type=MESH,
-                )
-            )
-        if k < chips:
-            sends.append(
-                pltpu.make_async_remote_copy(
-                    src_ref=ent, dst_ref=dst_out.at[r], send_sem=row_s.at[k], recv_sem=row_r.at[k],
-                    device_id=(((chip + k) % chips) * 2 + core, c), device_id_type=MESH,
-                )
-            )
-    sends.append(
-        pltpu.make_async_remote_copy(
-            src_ref=ent, dst_ref=dst_out.at[r], send_sem=pair_s.at[0], recv_sem=pair_r.at[0],
-            device_id=(mate, c), device_id_type=MESH,
+    def copy(k, src, dst, peer):
+        return pltpu.make_async_remote_copy(
+            src_ref=src, dst_ref=dst, send_sem=send_sem.at[k], recv_sem=recv_sem.at[k],
+            device_id=peer, device_id_type=MESH,
         )
-    )
-    for send in sends:
-        send.start()
+
+    own = lambda p: ent.at[p]
+    col = lambda i, p: src_out.at[i, p]
+    row = lambda i, p: dst_out.at[i, p]
+    started = []
+
+    def start(k, src, dst, peer):
+        move = copy(k, src, dst, peer)
+        move.start()
+        started.append(move)
+
+    def arrive(k, dst):
+        copy(k, own(0), dst, mate).wait_recv()
+
+    start(0, own(0), col(c, 0), above)
+    start(3, own(1), col(c, 1), below)
+    start(6, own(0), row(r, 0), xp)
+    start(9, own(1), row(r, 1), yp)
+    start(1, own(1), col(c, 1), above)
+    start(2, own(0), col(c, 0), below)
+    start(7, own(1), row(r, 1), xp)
+    start(8, own(0), row(r, 0), yp)
+    start(12, own(0), row(r, 0), mate)
+    start(19, own(1), row(r, 1), mate)
     local = [
         pltpu.make_async_copy(ent, src_out.at[c], loc_sem.at[0]),
         pltpu.make_async_copy(ent, dst_out.at[r], loc_sem.at[1]),
     ]
-    for copy in local:
-        copy.start()
-    relays = []
-    for k in range(1, chips):
-        origin = ((chip + chips - k) % chips) * 2 + core
-        pltpu.make_async_remote_copy(
-            src_ref=ent, dst_ref=dst_out.at[origin], send_sem=row_s.at[k], recv_sem=row_r.at[k],
-            device_id=(mate, c), device_id_type=MESH,
-        ).wait_recv()
-        relay = pltpu.make_async_remote_copy(
-            src_ref=dst_out.at[origin], dst_ref=dst_out.at[origin], send_sem=pair_s.at[k], recv_sem=pair_r.at[k],
-            device_id=(mate, c), device_id_type=MESH,
-        )
-        relay.start()
-        relays.append(relay)
-    for k in range(1, n_col):
-        pltpu.make_async_remote_copy(
-            src_ref=ent, dst_ref=src_out.at[(c + n_col - k) % n_col], send_sem=col_s.at[k], recv_sem=col_r.at[k],
-            device_id=(mate, c), device_id_type=MESH,
-        ).wait_recv()
-    for send in sends:
-        send.wait_send()
-    sends[-1].wait_recv()
-    for relay in relays:
-        relay.wait()
-    for copy in local:
-        copy.wait()
+    for move in local:
+        move.start()
+    arrive(0, col(down, 0))
+    start(4, col(down, 0), col(down, 0), above)
+    arrive(3, col(up, 1))
+    start(5, col(up, 1), col(up, 1), below)
+    arrive(6, row(xr, 0))
+    start(10, row(xr, 0), row(xr, 0), yp)
+    arrive(9, row(yr, 1))
+    start(11, row(yr, 1), row(yr, 1), xp)
+    start(13, row(xr, 0), row(xr, 0), mate)
+    start(16, row(yr, 1), row(yr, 1), mate)
+    arrive(7, row(xr, 1))
+    start(14, row(xr, 1), row(xr, 1), mate)
+    arrive(8, row(yr, 0))
+    start(15, row(yr, 0), row(yr, 0), mate)
+    arrive(10, row(dr, 0))
+    start(17, row(dr, 0), row(dr, 0), mate)
+    arrive(11, row(dr, 1))
+    start(18, row(dr, 1), row(dr, 1), mate)
+    arrive(1, col(down, 1))
+    arrive(2, col(up, 0))
+    arrive(4, col(across, 0))
+    arrive(5, col(across, 1))
+    twin = lambda yy, xx: (yy * 2 + xx) * 2 + (1 - core)
+    mx, my, md = twin(y, 1 - x), twin(1 - y, x), twin(1 - y, 1 - x)
+    arrive(12, row(mate[0], 0))
+    arrive(19, row(mate[0], 1))
+    arrive(13, row(mx, 0))
+    arrive(14, row(mx, 1))
+    arrive(15, row(my, 0))
+    arrive(16, row(my, 1))
+    arrive(17, row(md, 0))
+    arrive(18, row(md, 1))
+    for move in started:
+        move.wait_send()
+    for move in local:
+        move.wait()
 
 
 def spread(n_row, n_col, ent):
-    chips = n_row // 2
     dma = pltpu.SemaphoreType.DMA
     return pl.pallas_call(
-        functools.partial(spread_kernel, n_row, n_col),
+        functools.partial(spread_kernel, n_col),
         name="spread",
         out_shape=(
             jax.ShapeDtypeStruct((n_col,) + ent.shape, ent.dtype),
@@ -99,79 +115,90 @@
         ),
         in_specs=[pl.BlockSpec(memory_space=pltpu.VMEM)],
         out_specs=(pl.BlockSpec(memory_space=pltpu.HBM), pl.BlockSpec(memory_space=pltpu.HBM)),
-        scratch_shapes=[
-            dma((2,)), dma((n_col,)), dma((n_col,)), dma((chips,)), dma((chips,)), dma((chips,)), dma((chips,)),
-        ],
+        scratch_shapes=[dma((2,)), dma((20,)), dma((20,))],
         compiler_params=pltpu.CompilerParams(collective_id=0, has_side_effects=True),
     )(ent)
 
 
-def gather_sum_kernel(n_row, n_col, acc, out, pair_buf, sums, got, pair_s, pair_r, far_s, far_r):
+def gather_sum_kernel(n_col, acc, out, pair_buf, sa, sb, a1, b1, ta, tb, a2, b2, tot, got, send_sem, recv_sem):
     r, c = lax.axis_index("row"), lax.axis_index("col")
-    chips = n_row // 2
     chip, core = r // 2, r % 2
-    mate = chip * 2 + (1 - core)
-    steps = [(a, b) for a in range(chips) for b in range(n_col) if a or b]
-    goal = lambda a, b: (((chip + a) % chips) * 2 + core, (c + b) % n_col)
+    y, x = chip // 2, chip % 2
+    row_of = lambda yy, xx: (yy * 2 + xx) * 2 + core
+    mate = (chip * 2 + (1 - core), c)
+    xp, yp = (row_of(y, 1 - x), c), (row_of(1 - y, x), c)
+    ring = [(r, (c + b) % n_col) for b in range(1, n_col)]
 
     barrier = pltpu.get_barrier_semaphore()
-    for a, b in steps:
-        pl.semaphore_signal(barrier, inc=1, device_id=goal(a, b), device_id_type=MESH)
-    pl.semaphore_signal(barrier, inc=1, device_id=(mate, c), device_id_type=MESH)
-    pl.semaphore_wait(barrier, len(steps) + 1)
-
-    pairs = []
-    for j in range(chips):
-        copy = pltpu.make_async_remote_copy(
-            src_ref=acc.at[j, 1 - core], dst_ref=pair_buf.at[j], send_sem=pair_s.at[j], recv_sem=pair_r.at[j],
-            device_id=(mate, c), device_id_type=MESH,
+    peers = [mate, xp, yp] + ring
+    for peer in peers:
+        pl.semaphore_signal(barrier, inc=1, device_id=peer, device_id_type=MESH)
+    pl.semaphore_wait(barrier, len(peers))
+
+    started = []
+
+    def start(k, src, dst, peer):
+        move = pltpu.make_async_remote_copy(
+            src_ref=src, dst_ref=dst, send_sem=send_sem.at[k], recv_sem=recv_sem.at[k],
+            device_id=peer, device_id_type=MESH,
         )
-        copy.start()
-        pairs.append(copy)
-    for j in range(chips):
-        pairs[j].wait_recv()
-        sums[j] = acc[j, core] + pair_buf[j]
-    sends = []
-    for a, b in steps:
-        send = pltpu.make_async_remote_copy(
-            src_ref=sums.at[(chip + a) % chips, (c + b) % n_col], dst_ref=got.at[a, b],
-            send_sem=far_s.at[a, b], recv_sem=far_r.at[a, b],
-            device_id=goal(a, b), device_id_type=MESH,
-        )
-        send.start()
-        sends.append(send)
-    total = sums[chip, c]
-    for send, (a, b) in zip(sends, steps):
-        send.wait_recv()
-        total = total + got[a, b]
+        move.start()
+        started.append(move)
+        return move
+
+    spots = [(yy, xx) for yy in range(2) for xx in range(2)]
+    pairs = [start(k, acc.at[yy, xx, 1 - core], pair_buf.at[yy, xx], mate) for k, (yy, xx) in enumerate(spots)]
+    for move, (yy, xx) in zip(pairs, spots):
+        move.wait_recv()
+        whole = acc[yy, xx, core] + pair_buf[yy, xx]
+        sa[yy, xx] = whole[:, :, :WIDE]
+        sb[yy, xx] = whole[:, :, WIDE:]
+    move_a = start(4, sa.at[:, 1 - x], a1, xp)
+    move_b = start(5, sb.at[1 - y], b1, yp)
+    move_a.wait_recv()
+    ta[0] = sa[1 - y, x] + a1[1 - y]
+    next_a = start(6, ta.at[0], a2, yp)
+    ta[1] = sa[y, x] + a1[y]
+    move_b.wait_recv()
+    tb[0] = sb[y, 1 - x] + b1[1 - x]
+    next_b = start(7, tb.at[0], b2, xp)
+    tb[1] = sb[y, x] + b1[x]
+    next_a.wait_recv()
+    tot[:, :, :WIDE] = ta[1] + a2[...]
+    next_b.wait_recv()
+    tot[:, :, WIDE:] = tb[1] + b2[...]
+    hops = [start(8 + b, tot.at[peer[1]], got.at[b], peer) for b, peer in enumerate(ring)]
+    total = tot[c]
+    for b, move in enumerate(hops):
+        move.wait_recv()
+        total = total + got[b]
     width = out.shape[2]
     out[0] = total[:, :width]
     out[1] = total[:, WIDE : WIDE + width]
-    for send in sends:
-        send.wait_send()
-    for copy in pairs:
-        copy.wait_send()
+    for move in started:
+        move.wait_send()
 
 
 def gather_sum(n_row, n_col, acc, dim):
-    chips = n_row // 2
     rows = acc.shape[0] // (n_row * n_col)
     wide = acc.shape[1]
     dma = pltpu.SemaphoreType.DMA
+    block = lambda *lead: pltpu.VMEM(lead + (n_col, rows, WIDE), F32)
     return pl.pallas_call(
-        functools.partial(gather_sum_kernel, n_row, n_col),
+        functools.partial(gather_sum_kernel, n_col),
         name="gather_sum",
         out_shape=jax.ShapeDtypeStruct((2, rows, dim), F32),
         in_specs=[pl.BlockSpec(memory_space=pltpu.VMEM)],
         out_specs=pl.BlockSpec(memory_space=pltpu.VMEM),
         scratch_shapes=[
-            pltpu.VMEM((chips, n_col, rows, wide), F32),
-            pltpu.VMEM((chips, n_col, rows, wide), F32),
-            pltpu.VMEM((chips, n_col, rows, wide), F32),
-            dma((chips,)), dma((chips,)), dma((chips, n_col)), dma((chips, n_col)),
+            pltpu.VMEM((2, 2, n_col, rows, wide), F32),
+            block(2, 2), block(2, 2), block(2), block(2), block(2), block(2), block(), block(),
+            pltpu.VMEM((n_col, rows, wide), F32),
+            pltpu.VMEM((n_col - 1, rows, wide), F32),
+            dma((7 + n_col,)), dma((7 + n_col,)),
         ],
         compiler_params=pltpu.CompilerParams(collective_id=1, has_side_effects=True),
-    )(acc.reshape(chips, 2, n_col, rows, wide))
+    )(acc.reshape(2, 2, 2, n_col, rows, wide))
 
 
 def edge_kernel(
@@ -239,18 +266,18 @@
 
         def pick(i, inner):
             got = []
-            for u in range(8):
-                e = i * 8 + u
+            for u in range(16):
+                e = i * 16 + u
                 a = pl.multiple_of(src_i[g * group + e] * 4, 4)
                 b = pl.multiple_of(dst_i[g * group + e] * 4, 4)
                 k = pl.multiple_of(rel_i[g * group + e] * 4, 4)
                 got.append((s_tab[pl.ds(a, 4), :], o_tab[pl.ds(b, 4), :], w_tab[pl.ds(k, 4), :]))
-            for u in range(8):
-                at = pl.ds(pl.multiple_of((i * 8 + u) * 4, 4), 4)
+            for u in range(16):
+                at = pl.ds(pl.multiple_of((i * 16 + u) * 4, 4), 4)
                 gs[at, :], go[at, :], gw[at, :] = got[u]
             return inner
 
-        lax.fori_loop(0, group // 8, pick, 0)
+        lax.fori_loop(0, group // 16, pick, 0)
 
         qrows = 32
 
@@ -361,7 +388,7 @@
     dim = entities.shape[2]
     ent = entities.shape[1]
     pad = ((0, 0), (0, 0), (0, WIDE - dim))
-    if (n_row + n_col) * ent * 4 * LANE * 4 > 36 * 2**20:
+    if n_row != 8 or n_col != 4 or (n_row + n_col) * ent * 4 * LANE * 4 > 36 * 2**20:
         return wide_body(entities, relations, src_index, dst_index, rel_index, neg_block)
     src_all, dst_all = spread(n_row, n_col, jnp.pad(entities, pad))
     edge_loss, acc = edge_terms(

time: 201 us -> 174 us (0.87)
  Pallas kernels: 194 us -> 167 us
    pallas_call x2, Pallas kernels: 128 us -> 101 us  [the longest x1 74.2 us: spread(): pl.pallas_call(functools.partial(spread_kernel, n_col), name='spread', ou...]
where the time goes in v2:
time: 174 us
  Pallas kernels  167 us (96%)
  local copies, waits for them, and re-layouts  5.89 us (3%)
    pallas_call x1, Pallas kernels, spread(): pl.pallas_call(functools.partial(spread_kernel, n_col), name='spread', ou...  74.2 us
    pallas_call x1, Pallas kernels, edge_terms(): pl.pallas_call(functools.partial(edge_kernel, group), name='edge_terms',...  65.6 us
    pallas_call x1, Pallas kernels, gather_sum(): pl.pallas_call(functools.partial(gather_sum_kernel, n_col), name='gather_...  27.1 us
    unnamed x5, local copies, waits for them, and re-layouts  3.5 us

profile of v2, /device:TPU:0, one launch (start us, length us, event | category | flops | bytes accessed | tf_op | source)
XLA Modules:
  0.0 173.5 jit_solution(5333554919482069002)
XLA Ops:
  0.6 0.0 copy-start
  0.6 1.5 copy.9
  2.2 1.2 pad.8.ent
  3.4 0.0 copy-done
  3.4 0.5 copy.8
  3.9 1.2 pad.7.rel_tab
  5.1 74.2 %spread.1 = (bf16[4,2,1024,256]{3,2,1,0:T(8,128)(2,1)}, bf16[8,2,1024,256]{3,2,1,0:T(8,128)(2,1)}) custom-call(bf16[2,1024,256]{2,1,0:T(8,128)(2,1)} %pad.8.ent), custom_call_target="tpu_custom_call" | custom-call | tf_op jit(solution)/shard_map/spread/pallas_call | solution.py:109
  79.3 65.6 %edge_terms.1 = (f32[32,128]{1,0:T(8,128)}, f32[1024,512]{1,0:T(8,128)}) custom-call(s32[4096]{0:T(1024)} %src_i.1, s32[4096]{0:T(1024)} %dst_i.1, s32[4096]{0:T(1024)} %rel_i.1, s32[8]{0:T(128)} %neg_i.1, s32[1,4096]{1,0:T(1,128)} %bitcast.4, bf16[2,1024,256]{2,1,0:T(8,128)(2,1)} %pad.7.rel_tab, bf16[4,2,1024,256]{3,2,1,0:T(8,128)(2,1)} %get-tuple-element.6.src_all, ...), custom_call_target="tpu_custom_call" | custom-call | tf_op jit(solution)/shard_map/edge_terms/pallas_call | solution.py:357
  144.9 27.1 %gather_sum.1 = f32[2,32,200]{2,1,0:T(8,128)} custom-call(f32[2,2,2,4,32,512]{5,4,3,2,1,0:T(8,128)} %bitcast.3), custom_call_target="tpu_custom_call" | custom-call | tf_op jit(solution)/shard_map/gather_sum/pallas_call | solution.py:187
  172.1 1.5 copy.11
Async XLA Ops:
  0.6 2.7 %copy-start = (bf16[2,1024,200]{1,2,0:T(8,128)(2,1)S(1)}, bf16[2,1024,200]{1,2,0:T(8,128)(2,1)}, u32[]{:S(2)}) copy-start(bf16[2,1024,200]{1,2,0:T(8,128)(2,1)} %param.7) | copy-start | bytes 2457604
